TPU v7x, 256 devices: a whole 4x4x8 slice. The times are simulated.
256 devices in a mesh: ep: 8 (over z_lo, core), fsdp: 32 (over z_hi, y, x).
Axes of the slice: x: 4, y: 4, z: 8 (z_hi: 2, z_lo: 4; z = z_hi * 4 + z_lo), core: 2. Of those that a mesh axis runs over, the one named last changes fastest.
Arguments:
- train_down: float32 [8, 14336, 4096], P('ep', None, 'fsdp'), may hold values from -0.09375 to 0.09375
- router_weight: float32 [4096, 8], P('fsdp', 'ep'), may hold values from -0.09375 to 0.09375
- router_gain: float32 [4096], P('fsdp'), may hold values from 0.25 to 1.75
Outputs:
- ready_down: bfloat16 [8, 14336, 4096], P('ep', 'fsdp')
- scale_down: float32 [8, 14336], P('ep', 'fsdp')
- serve_router: bfloat16 [4096, 8], replicated
All inputs are finite; a program needn't handle non-finite values.
Results may differ from a plain program's by a relative error of at most 0.001.
Values may be sent and summed in bfloat16 or wider, within the bound.
A program may use at most 64 MiB of HBM per device.

v0:
```python
import functools

import jax
import jax.numpy as jnp
from jax import lax
from jax.sharding import Mesh
from jax.sharding import PartitionSpec as P

FSDP = ("fsdp_0", "fsdp_1", "fsdp_2")


def by_axis(x, axes):
    return functools.reduce(lax.psum, axes, x)


def split_up(x, dim, length):
    lengths = x.shape
    tiles = x.reshape(*lengths[:dim], length, lengths[dim] // length, *lengths[dim + 1 :])
    return jnp.moveaxis(tiles, dim, 0)


def piece_ends(length, count):
    turn = length // count
    if turn >= 8:
        turn -= turn % 8
    return [turn * k for k in range(1, count)]


def in_order(tiles, dim):
    tiles = jnp.moveaxis(tiles, 0, dim)
    lengths = tiles.shape
    return tiles.reshape(*lengths[:dim], lengths[dim] * lengths[dim + 1], *lengths[dim + 2 :])


def cut_exchange(x, axis, pieces, split_dim, concat_dim):
    tiles = split_up(x, split_dim, lax.axis_size(axis))
    cut = max(range(1, max(2, tiles.ndim - 1)), key=lambda d: tiles.shape[d])
    done = []
    for share in jnp.split(tiles, piece_ends(tiles.shape[cut], pieces), axis=cut):
        if share.size:
            done.append(lax.all_to_all(share, axis, split_axis=0, concat_axis=0, tiled=True))
    return in_order(jnp.concatenate(done, axis=cut), concat_dim)


def from_everyone(x, axis):
    copies = jnp.broadcast_to(x, (lax.axis_size(axis), *x.shape))
    return lax.all_to_all(copies, axis, split_axis=0, concat_axis=0, tiled=True)


def gathered_copies(x, axis, dim):
    return in_order(from_everyone(x, axis), dim)


def body(train_down, router_weight, router_gain):
    total_down = by_axis(jnp.sum(train_down * train_down, axis=2), FSDP)
    scale_down = jnp.sqrt(total_down)
    narrow_down = (train_down / jnp.expand_dims(scale_down, 2)).astype(jnp.bfloat16)
    ready_down = cut_exchange(narrow_down, FSDP, 2, 1, 2)
    scale_down = lax.dynamic_slice_in_dim(
        scale_down, lax.axis_index(FSDP) * ready_down.shape[1], ready_down.shape[1], axis=1
    )
    part_router = (router_weight * router_gain[:, None]).astype(jnp.bfloat16)
    row_router = gathered_copies(part_router, FSDP, 0)
    serve_router = gathered_copies(row_router, "ep", 1)
    return (ready_down, scale_down, serve_router)


def solution(mesh):
    torus = Mesh(
        mesh.devices.reshape(mesh.shape["ep"], 2, 4, 4), ("ep", "fsdp_0", "fsdp_1", "fsdp_2")
    )
    in_specs = (P("ep", None, FSDP), P(FSDP, "ep"), P(FSDP))
    out_specs = (P("ep", FSDP, None), P("ep", FSDP), P())
    return jax.shard_map(body, mesh=torus, in_specs=in_specs, out_specs=out_specs, check_vma=False)
```

profile of v0, /device:TPU:32, one launch (start us, length us, event | category | flops | bytes accessed | tf_op | source)
XLA Modules:
  0.0 191.6 jit_solution(14340416555964060221)
XLA Ops:
  0.6 0.7 fusion.1
  1.3 0.6 broadcast_in_dim.11
  1.9 13.0 %all-to-all-start.2 = ((bf16[32,128,1]{1,2,0:T(2,128)(2,1)}), bf16[32,128,1]{1,2,0:T(2,128)(2,1)S(1)}, u32[]{:S(2)}, u32[]{:S(2)}) async-start(bf16[32,128,1]{1,2,0:T(2,128)(2,1)} %broadcast_in_dim.11), calls=%async_computation.2 | async-start | bytes 32768 | tf_op jit(solution)/shard_map/all_to_all | solution.py:47
  15.0 4.2 %multiply_reduce_fusion = f32[14336]{0:T(1024)S(1)} fusion(f32[1,14336,128]{2,1,0:T(8,128)} %param.3), kind=kLoop, calls=%fused_computation.1 | loop fusion | flops 3655680 | bytes 7397376 | tf_op jit(solution)/shard_map/reduce_sum | solution.py:55
  19.2 17.1 %psum.21 = f32[1,14336]{1,0:T(1,128)S(1)} all-reduce(f32[1,14336]{1,0:T(1,128)S(1)} %bitcast.29), channel_id=1, replica_groups=mesh['ep'=8,'fsdp_0'=2,'fsdp_1'=4,'fsdp_2'=4] {'fsdp_0'}, use_global_device_ids=true, to_apply=%region_1.0 | all-reduce | flops 14336 | bytes 114688 | tf_op jit(solution)/shard_map/psum | solution.py:13
  36.3 17.4 %psum.22 = f32[1,14336]{1,0:T(1,128)S(1)} all-reduce(f32[1,14336]{1,0:T(1,128)S(1)} %psum.21), channel_id=1, replica_groups=mesh['ep'=8,'fsdp_0'=2,'fsdp_1'=4,'fsdp_2'=4] {'fsdp_1'}, use_global_device_ids=true, to_apply=%region_2.0 | all-reduce | flops 14336 | bytes 114688 | tf_op jit(solution)/shard_map/psum | solution.py:13
  53.7 17.5 %psum.23 = f32[1,14336]{1,0:T(1,128)S(1)} all-reduce(f32[1,14336]{1,0:T(1,128)S(1)} %psum.22), channel_id=1, replica_groups=mesh['ep'=8,'fsdp_0'=2,'fsdp_1'=4,'fsdp_2'=4] {'fsdp_2'}, use_global_device_ids=true, to_apply=%region_3.0 | all-reduce | flops 14336 | bytes 114688 | tf_op jit(solution)/shard_map/psum | solution.py:13
  71.1 0.1 sqrt.3
  71.2 8.8 %divide_convert_fusion = bf16[1,14336,128]{2,1,0:T(8,128)(2,1)} fusion(f32[1,14336,128]{2,1,0:T(8,128)} %param.3, f32[14336]{0:T(1024)S(1)} %bitcast.28), kind=kLoop, calls=%fused_computation | loop fusion | flops 3670016 | bytes 11067392 | tf_op jit(solution)/shard_map/convert_element_type | solution.py:57
  80.0 0.0 all-to-all-done.2
  80.0 0.1 reduce.1
  80.1 0.1 broadcast_bitcast_fusion
  80.2 0.5 broadcast.4
  80.7 1.0 reduce.2
  81.7 0.7 reshape.26
  82.3 4.3 %all-to-all-start.3 = ((bf16[8,2,2048]{2,1,0:T(2,128)(2,1)}), bf16[8,2,2048]{2,1,0:T(2,128)(2,1)S(1)}, u32[]{:S(2)}, u32[]{:S(2)}) async-start(bf16[8,2,2048]{2,1,0:T(2,128)(2,1)} %reshape.26), calls=%async_computation.3 | async-start | bytes 131072 | tf_op jit(solution)/shard_map/all_to_all | solution.py:47
  86.6 4.1 %fusion.2 = (bf16[32,1,224,128]{3,2,1,0:T(8,128)(2,1)}, bf16[32,1,224,128]{3,2,1,0:T(8,128)(2,1)}) fusion(bf16[32,1,448,128]{3,2,1,0:T(8,128)(2,1)} %bitcast.26), kind=kLoop, calls=%fused_computation.9 | loop fusion | bytes 7340032 | tf_op jit(solution)/shard_map/split | solution.py:39
  90.7 0.6 all-to-all-done.3
  91.3 52.9 %all_to_all.20 = bf16[32,1,224,128]{3,2,1,0:T(8,128)(2,1)S(1)} all-to-all(bf16[32,1,224,128]{3,2,1,0:T(8,128)(2,1)} %get-tuple-element.3), channel_id=1, replica_groups=mesh['ep'=8,'fsdp_0'=2,'fsdp_1'=4,'fsdp_2'=4] {'fsdp_0','fsdp_1','fsdp_2'}, dimensions={0} | all-to-all | bytes 3670016 | tf_op jit(solution)/shard_map/all_to_all | solution.py:41
  144.1 4.7 %all-to-all-start.1 = ((bf16[32,1,224,128]{3,2,1,0:T(8,128)(2,1)}), bf16[32,1,224,128]{3,2,1,0:T(8,128)(2,1)}, u32[]{:S(2)}, u32[]{:S(2)}) async-start(bf16[32,1,224,128]{3,2,1,0:T(8,128)(2,1)} %get-tuple-element.4), calls=%async_computation.1 | async-start | bytes 3670016 | tf_op jit(solution)/shard_map/all_to_all | solution.py:41
  148.9 0.7 constant_dynamic-slice_fusion
  149.5 0.1 reshape.27
  149.6 0.7 copy.15
  150.3 38.0 %all-to-all-done.1 = bf16[32,1,224,128]{3,2,1,0:T(8,128)(2,1)} async-done(((bf16[32,1,224,128]{3,2,1,0:T(8,128)(2,1)}), bf16[32,1,224,128]{3,2,1,0:T(8,128)(2,1)}, u32[]{:S(2)}, u32[]{:S(2)}) %all-to-all-start.1) | async-done | bytes 1835040 | tf_op jit(solution)/shard_map/all_to_all | solution.py:41
  188.3 3.3 %copy_bitcast_fusion = bf16[1,448,4096]{2,1,0:T(8,128)(2,1)} fusion(bf16[32,1,224,128]{3,2,1,0:T(8,128)(2,1)} %all-to-all-done.1, bf16[32,1,224,128]{3,2,1,0:T(8,128)(2,1)S(1)} %all_to_all.20), kind=kLoop, calls=%fused_computation.2 | loop fusion | flops 7340032 | bytes 7340032 | tf_op jit(solution)/shard_map/reshape | solution.py:32
Async XLA Ops:
  1.9 78.1 %all-to-all-start.2 = ((bf16[32,128,1]{1,2,0:T(2,128)(2,1)}), bf16[32,128,1]{1,2,0:T(2,128)(2,1)S(1)}, u32[]{:S(2)}, u32[]{:S(2)}) async-start(bf16[32,128,1]{1,2,0:T(2,128)(2,1)} %broadcast_in_dim.11), calls=%async_computation.2 | async-start | bytes 32768 | tf_op jit(solution)/shard_map/all_to_all | solution.py:47
  82.3 8.9 %all-to-all-start.3 = ((bf16[8,2,2048]{2,1,0:T(2,128)(2,1)}), bf16[8,2,2048]{2,1,0:T(2,128)(2,1)S(1)}, u32[]{:S(2)}, u32[]{:S(2)}) async-start(bf16[8,2,2048]{2,1,0:T(2,128)(2,1)} %reshape.26), calls=%async_computation.3 | async-start | bytes 131072 | tf_op jit(solution)/shard_map/all_to_all | solution.py:47
  144.1 44.2 %all-to-all-start.1 = ((bf16[32,1,224,128]{3,2,1,0:T(8,128)(2,1)}), bf16[32,1,224,128]{3,2,1,0:T(8,128)(2,1)}, u32[]{:S(2)}, u32[]{:S(2)}) async-start(bf16[32,1,224,128]{3,2,1,0:T(8,128)(2,1)} %get-tuple-element.4), calls=%async_computation.1 | async-start | bytes 3670016 | tf_op jit(solution)/shard_map/all_to_all | solution.py:41
where the time goes:
time: 192 us
  blocking collectives  105 us (55%)
  waiting for transfers between devices  38.6 us (20%)
  starting transfers between devices  22 us (11%)
  other arithmetic  18 us (9%)
  local copies, waits for them, and re-layouts  7.51 us (4%)
    all_to_all x1, blocking collectives, cut_exchange(): lax.all_to_all(share, axis, split_axis=0, concat_axis=0, tiled=True)  52.9 us
    psum x3, blocking collectives, by_axis(): return functools.reduce(lax.psum, axes, x)  51.9 us
    all_to_all x1, waiting for transfers between devices, cut_exchange(): lax.all_to_all(share, axis, split_axis=0, concat_axis=0, tiled=True)  38 us
    all_to_all x2, starting transfers between devices, from_everyone(): return lax.all_to_all(copies, axis, split_axis=0, concat_axis=0, tiled=True)  17.3 us
    convert_element_type x1, other arithmetic, body(): (train_down / jnp.expand_dims(scale_down, 2)).astype(jnp.bfloat16)  8.78 us
    all_to_all x1, starting transfers between devices, cut_exchange(): lax.all_to_all(share, axis, split_axis=0, concat_axis=0, tiled=True)  4.72 us
    reduce_sum x1, other arithmetic, body(): total_down = by_axis(jnp.sum(train_down * train_down, axis=2), FSDP)  4.19 us
    split x1, local copies, waits for them, and re-layouts, cut_exchange(): jnp.split(tiles, piece_ends(tiles.shape[cut], pieces), axis=cut)  4.11 us
  transfers between devices with their start and end apart: 3, of which 2 were waited for; matrix products, arithmetic and copies ran while one was open for 10% of the time, Pallas kernels for 0%

commit v1 on v0

v1 whole, which is shorter than its diff:
```python
import jax
import jax.numpy as jnp
from jax import lax
from jax.experimental import pallas as pl
from jax.experimental.pallas import tpu as pltpu
from jax.sharding import PartitionSpec as P

MESH = pl.DeviceIdType.MESH
N = 32
EP = 8
ROWS = 448
COLS = 128
STORES = 7
CUTS = (0, 64, 192, 320, 448)


def peer(k):
    f = lax.axis_index("fsdp")
    h = (f // 16 + k // 16) % 2
    y = ((f // 4) % 4 + (k // 4) % 4) % 4
    x = (f % 4 + k % 4) % 4
    return h * 16 + y * 4 + x


def send(src, dst, send_sem, recv_sem, device):
    return pltpu.make_async_remote_copy(
        src_ref=src,
        dst_ref=dst,
        send_sem=send_sem,
        recv_sem=recv_sem,
        device_id=device,
        device_id_type=MESH,
    )


def drain(ref, sem):
    pltpu.make_async_copy(ref, ref, sem).wait()


def eye():
    return lax.broadcasted_iota(jnp.int32, (128, 128), 0) == lax.broadcasted_iota(jnp.int32, (128, 128), 1)


def to_lanes(column):
    n = column.shape[0]
    return jnp.sum(jnp.where(eye()[:n], column, 0.0), axis=0, keepdims=True)


def to_column(row, start, n):
    return jnp.sum(jnp.where(eye()[start : start + n], row, 0.0), axis=1, keepdims=True)


def exchange(
    train, weight, gain, ready, scale, router,
    x, small, part, parts, inverse, inverses, columns, rows16,
    load_sem, send_sem, recv_sem,
):
    e, f = lax.axis_index("ep"), lax.axis_index("fsdp")

    barrier = pltpu.get_barrier_semaphore()

    @pl.loop(1, N)
    def _(k):
        pl.semaphore_signal(barrier, inc=1, device_id={"ep": e, "fsdp": peer(k)}, device_id_type=MESH)

    @pl.loop(1, EP)
    def _(k):
        pl.semaphore_signal(barrier, inc=1, device_id={"ep": (e + k) % EP, "fsdp": f}, device_id_type=MESH)

    def load(to):
        return pltpu.make_async_copy(train.at[to], x.at[to], load_sem.at[to])

    @pl.loop(0, N)
    def _(to):
        load(to).start()

    loads = [pltpu.make_async_copy(ref, small.at[k], load_sem.at[N + k]) for k, ref in enumerate((weight, gain))]
    for copy in loads:
        copy.start()
    for copy in loads:
        copy.wait()
    routed = (small[0] * small[1]).astype(jnp.bfloat16).astype(jnp.float32)

    @pl.loop(0, N)
    def _(to):
        load(to).wait()
        sums = []
        for k in range(4):
            block = x[to, 128 * k : min(128 * k + 128, ROWS), :]
            sums.append(to_lanes(jnp.sum(block * block, axis=1, keepdims=True)))
        part[to] = jnp.concatenate(sums + [routed, jnp.zeros((3, 128), jnp.float32)], axis=0)

    pl.semaphore_wait(barrier, N - 1 + EP - 1)

    def to_all(src_of, dst, number):
        @pl.loop(1, N)
        def _(k):
            to = peer(k)
            send(src_of(to), dst, send_sem.at[number], recv_sem.at[number], {"ep": e, "fsdp": to}).start()

    to_all(lambda to: part.at[to], parts.at[f], 0)
    parts[f] = part[f]
    drain(parts.at[pl.ds(0, N - 1)], recv_sem.at[0])

    total = jnp.sum(parts[:, 0:4, :], axis=0)
    root = jnp.sqrt(total)
    inverse[...] = jnp.concatenate([1.0 / root, jnp.zeros((4, 128), jnp.float32)], axis=0)
    to_all(lambda to: inverse, inverses.at[f], 1)
    inverses[f] = inverse[...]

    columns[e] = parts[:, 4, :]

    @pl.loop(1, EP)
    def _(k):
        send(columns.at[e], columns.at[e], send_sem.at[2], recv_sem.at[2], {"ep": (e + k) % EP, "fsdp": f}).start()

    for k in range(4):
        n = min(128, ROWS - 128 * k)
        scale[:, 128 * k : 128 * k + n] = root[k : k + 1, :n]

    drain(inverses.at[pl.ds(0, N - 1)], recv_sem.at[1])

    mine = pl.ds(pl.multiple_of(f * COLS, COLS), COLS)
    for first, last in zip(CUTS[:-1], CUTS[1:]):

        def ready_rows(to):
            blocks = []
            row = first
            while row < last:
                k, start = row // 128, row % 128
                n = min(128 - start, last - row)
                factor = to_column(inverses[to, k : k + 1, :], start, n)
                blocks.append((x[to, row : row + n, :] * factor).astype(jnp.bfloat16))
                row += n
            return jnp.concatenate(blocks, axis=0) if len(blocks) > 1 else blocks[0]

        @pl.loop(1, N)
        def _(k):
            to = peer(N - k)
            rows16[to, first:last, :] = ready_rows(to)
            send(
                rows16.at[to, pl.ds(first, last - first)],
                ready.at[pl.ds(first, last - first), mine],
                send_sem.at[3],
                recv_sem.at[3],
                {"ep": e, "fsdp": to},
            ).start()

        ready[first:last, mine] = ready_rows(f)

    drain(columns.at[pl.ds(0, EP - 1)], recv_sem.at[2])
    for k in range(N):
        router[:, 128 * k : 128 * k + 128] = columns[:, k, :].astype(jnp.bfloat16)

    drain(rows16.at[pl.ds(0, N - 1)], recv_sem.at[3])
    drain(parts.at[pl.ds(0, N - 1)], send_sem.at[0])
    drain(inverses.at[pl.ds(0, N - 1)], send_sem.at[1])
    drain(columns.at[pl.ds(0, EP - 1)], send_sem.at[2])
    drain(rows16.at[pl.ds(0, N - 1)], send_sem.at[3])


def store(ready, scale, router, ready_out, scale_out, router_out, sem):
    rows = ROWS // STORES
    copies = [pltpu.make_async_copy(scale, scale_out, sem.at[0]), pltpu.make_async_copy(router, router_out, sem.at[1])]
    for k in range(STORES):
        piece = pl.ds(rows * k, rows)
        copies.append(pltpu.make_async_copy(ready.at[piece], ready_out.at[piece], sem.at[2 + k]))
    for copy in copies:
        copy.start()
    for copy in copies:
        copy.wait()


def body(train_down, router_weight, router_gain):
    ready, scale, router = pl.pallas_call(
        exchange,
        out_shape=(
            jax.ShapeDtypeStruct((ROWS, N * COLS), jnp.bfloat16),
            jax.ShapeDtypeStruct((1, ROWS), jnp.float32),
            jax.ShapeDtypeStruct((EP, N * COLS), jnp.bfloat16),
        ),
        in_specs=[pl.BlockSpec(memory_space=pltpu.HBM)] * 3,
        out_specs=[pl.BlockSpec(memory_space=pltpu.VMEM)] * 3,
        scratch_shapes=[
            pltpu.VMEM((N, ROWS, COLS), jnp.float32),
            pltpu.VMEM((2, 1, COLS), jnp.float32),
            pltpu.VMEM((N, 8, 128), jnp.float32),
            pltpu.VMEM((N, 8, 128), jnp.float32),
            pltpu.VMEM((8, 128), jnp.float32),
            pltpu.VMEM((N, 8, 128), jnp.float32),
            pltpu.VMEM((EP, N, 128), jnp.float32),
            pltpu.VMEM((N, ROWS, COLS), jnp.bfloat16),
            pltpu.SemaphoreType.DMA((N + 2,)),
            pltpu.SemaphoreType.DMA((4,)),
            pltpu.SemaphoreType.DMA((4,)),
        ],
        compiler_params=pltpu.CompilerParams(
            collective_id=0, has_side_effects=True, vmem_limit_bytes=32 * 2**20
        ),
        name="exchange",
    )(
        *(
            pltpu.with_memory_space_constraint(array, pltpu.HBM)
            for array in (
                train_down.reshape(N, ROWS, COLS),
                router_weight.reshape(1, COLS),
                router_gain.reshape(1, COLS),
            )
        )
    )
    ready, scale, router = pl.pallas_call(
        store,
        out_shape=(
            jax.ShapeDtypeStruct(ready.shape, ready.dtype),
            jax.ShapeDtypeStruct(scale.shape, scale.dtype),
            jax.ShapeDtypeStruct(router.shape, router.dtype),
        ),
        in_specs=[pl.BlockSpec(memory_space=pltpu.VMEM)] * 3,
        out_specs=[pl.BlockSpec(memory_space=pltpu.HBM)] * 3,
        scratch_shapes=[pltpu.SemaphoreType.DMA((2 + STORES,))],
        compiler_params=pltpu.CompilerParams(vmem_limit_bytes=2**20),
        name="store",
    )(ready, scale, router)
    return ready[None], scale, router.T


def solution(mesh):
    in_specs = (P("ep", None, "fsdp"), P("fsdp", "ep"), P("fsdp"))
    out_specs = (P("ep", "fsdp", None), P("ep", "fsdp"), P())
    return jax.shard_map(body, mesh=mesh, in_specs=in_specs, out_specs=out_specs, check_vma=False)
```

time: 192 us -> 117 us (0.61)
  the two profiles are of different devices: /device:TPU:32 before, /device:TPU:8 now
where the time goes in v1:
time: 117 us
  Pallas kernels  117 us (100%)
    pallas_call x1, Pallas kernels, body(): pl.pallas_call(exchange, out_shape=(jax.ShapeDtypeStruct((ROWS, N * COLS)...  115 us

profile of v1, /device:TPU:8, one launch (start us, length us, event | category | flops | bytes accessed | tf_op | source)
XLA Modules:
  0.0 117.3 jit_solution(6282596789864121478)
XLA Ops:
  0.6 114.8 %exchange.1 = (bf16[448,4096]{1,0:T(8,128)(2,1)S(1)}, f32[1,448]{1,0:T(1,128)S(1)}, bf16[8,4096]{1,0:T(8,128)(2,1)S(1)}) custom-call(f32[32,448,128]{2,1,0:T(8,128)} %bitcast.5, f32[1,128]{1,0:T(1,128)} %bitcast.6, f32[1,128]{1,0:T(1,128)} %bitcast.7), custom_call_target="tpu_custom_call" | custom-call | tf_op jit(solution)/shard_map/exchange/pallas_call | solution.py:175
  115.4 1.9 %store.1 = (bf16[448,4096]{1,0:T(8,128)(2,1)}, f32[1,448]{1,0:T(1,128)}, bf16[8,4096]{1,0:T(8,128)(2,1)}) custom-call(bf16[448,4096]{1,0:T(8,128)(2,1)S(1)} %get-tuple-element.9.ready, f32[1,448]{1,0:T(1,128)S(1)} %get-tuple-element.10.scale, bf16[8,4096]{1,0:T(8,128)(2,1)S(1)} %get-tuple-element.11.router), custom_call_target="tpu_custom_call" | custom-call | tf_op jit(solution)/shard_map/store/pallas_call | solution.py:211

commit v2 on v1

--- a/solution.py
+++ b/solution.py
@@ -11,7 +11,12 @@
 ROWS = 448
 COLS = 128
 STORES = 7
-CUTS = (0, 64, 192, 320, 448)
+HALF = N // 2
+CUTS = (0, 128, 256, 384, 448)
+EARLY = (48, 96)
+POWER = 15
+SPREAD = 2.0**8.4
+TINY = 1e-37
 
 
 def peer(k):
@@ -50,16 +55,43 @@
     return jnp.sum(jnp.where(eye()[start : start + n], row, 0.0), axis=1, keepdims=True)
 
 
+def code(block, squares):
+    u = block * (lax.rsqrt(jnp.maximum(squares, TINY)) * SPREAD)
+    u2 = u * u
+    u4 = u2 * u2
+    return (u4 * u4 * u4 * u2 * u).astype(jnp.bfloat16)
+
+
+def decode(coded, factor):
+    y = coded.astype(jnp.float32)
+    size = jnp.exp(jnp.log(jnp.maximum(jnp.abs(y), TINY)) * (1.0 / POWER)) * factor
+    return jnp.where(y > 0.0, size, jnp.where(y < 0.0, -size, 0.0 * factor)).astype(jnp.bfloat16)
+
+
+def blocks_of(first, last):
+    row = first
+    while row < last:
+        k, start = row // 128, row % 128
+        n = min(128 - start, last - row)
+        yield k, start, n
+        row += n
+
+
+def stacked(blocks):
+    return jnp.concatenate(blocks, axis=0) if len(blocks) > 1 else blocks[0]
+
+
 def exchange(
     train, weight, gain, ready, scale, router,
-    x, small, part, parts, inverse, inverses, columns, rows16,
-    load_sem, send_sem, recv_sem,
+    x, small, part, parts, inverse, inverses, columns, rows16, coded,
+    load_sem, send_sem, recv_sem, far_sem,
 ):
     e, f = lax.axis_index("ep"), lax.axis_index("fsdp")
+    partner = peer(HALF)
 
     barrier = pltpu.get_barrier_semaphore()
 
-    @pl.loop(1, N)
+    @pl.loop(1, HALF + 1)
     def _(k):
         pl.semaphore_signal(barrier, inc=1, device_id={"ep": e, "fsdp": peer(k)}, device_id_type=MESH)
 
@@ -71,8 +103,8 @@
         return pltpu.make_async_copy(train.at[to], x.at[to], load_sem.at[to])
 
     @pl.loop(0, N)
-    def _(to):
-        load(to).start()
+    def _(k):
+        load(peer((HALF + k) % N)).start()
 
     loads = [pltpu.make_async_copy(ref, small.at[k], load_sem.at[N + k]) for k, ref in enumerate((weight, gain))]
     for copy in loads:
@@ -81,31 +113,61 @@
         copy.wait()
     routed = (small[0] * small[1]).astype(jnp.bfloat16).astype(jnp.float32)
 
-    @pl.loop(0, N)
-    def _(to):
+    def squares(to, coded_rows):
         load(to).wait()
         sums = []
         for k in range(4):
             block = x[to, 128 * k : min(128 * k + 128, ROWS), :]
-            sums.append(to_lanes(jnp.sum(block * block, axis=1, keepdims=True)))
+            column = jnp.sum(block * block, axis=1, keepdims=True)
+            sums.append(to_lanes(column))
+            n = min(coded_rows - 128 * k, block.shape[0])
+            if n > 0:
+                rows16[to, 128 * k : 128 * k + n, :] = code(block[:n], column[:n])
         part[to] = jnp.concatenate(sums + [routed, jnp.zeros((3, 128), jnp.float32)], axis=0)
 
-    pl.semaphore_wait(barrier, N - 1 + EP - 1)
-
-    def to_all(src_of, dst, number):
-        @pl.loop(1, N)
+    squares(partner, ROWS)
+
+    @pl.loop(HALF + 1, N)
+    def _(k):
+        squares(peer(k), EARLY[-1])
+
+    @pl.loop(0, HALF)
+    def _(k):
+        squares(peer(k), 0)
+
+    pl.semaphore_wait(barrier, HALF + EP - 1)
+
+    pl.semaphore_signal(far_sem, inc=1, device_id={"ep": e, "fsdp": partner}, device_id_type=MESH)
+    send(rows16.at[partner], coded.at[f], send_sem.at[3], recv_sem.at[5], {"ep": e, "fsdp": partner}).start()
+
+    def to_each(start, stop, src_of, dst, number):
+        @pl.loop(start, stop)
         def _(k):
             to = peer(k)
             send(src_of(to), dst, send_sem.at[number], recv_sem.at[number], {"ep": e, "fsdp": to}).start()
 
-    to_all(lambda to: part.at[to], parts.at[f], 0)
+    to_each(1, HALF, lambda to: part.at[to], parts.at[f], 0)
+    pl.semaphore_wait(far_sem, 1)
+    to_each(HALF, N, lambda to: part.at[to], parts.at[f], 0)
+
+    def early(first, last):
+        rows = pl.ds(first, last - first)
+
+        @pl.loop(HALF + 1, N)
+        def _(k):
+            to = peer(k)
+            send(rows16.at[to, rows], coded.at[f, rows], send_sem.at[3], recv_sem.at[4], {"ep": e, "fsdp": to}).start()
+
+    early(0, EARLY[0])
     parts[f] = part[f]
     drain(parts.at[pl.ds(0, N - 1)], recv_sem.at[0])
 
     total = jnp.sum(parts[:, 0:4, :], axis=0)
     root = jnp.sqrt(total)
     inverse[...] = jnp.concatenate([1.0 / root, jnp.zeros((4, 128), jnp.float32)], axis=0)
-    to_all(lambda to: inverse, inverses.at[f], 1)
+    to_each(HALF, N, lambda to: inverse, inverses.at[f], 1)
+    to_each(1, HALF, lambda to: inverse, inverses.at[f], 1)
+    early(EARLY[0], EARLY[1])
     inverses[f] = inverse[...]
 
     columns[e] = parts[:, 4, :]
@@ -121,38 +183,53 @@
     drain(inverses.at[pl.ds(0, N - 1)], recv_sem.at[1])
 
     mine = pl.ds(pl.multiple_of(f * COLS, COLS), COLS)
-    for first, last in zip(CUTS[:-1], CUTS[1:]):
-
-        def ready_rows(to):
-            blocks = []
-            row = first
-            while row < last:
-                k, start = row // 128, row % 128
-                n = min(128 - start, last - row)
-                factor = to_column(inverses[to, k : k + 1, :], start, n)
-                blocks.append((x[to, row : row + n, :] * factor).astype(jnp.bfloat16))
-                row += n
-            return jnp.concatenate(blocks, axis=0) if len(blocks) > 1 else blocks[0]
-
-        @pl.loop(1, N)
+
+    def ready_rows(to, first, last):
+        return stacked(
+            [
+                (x[to, 128 * k + start : 128 * k + start + n, :] * to_column(inverses[to, k : k + 1, :], start, n)).astype(jnp.bfloat16)
+                for k, start, n in blocks_of(first, last)
+            ]
+        )
+
+    def exact(begin, end, first, last, number):
+        rows = pl.ds(first, last - first)
+
+        @pl.loop(begin, end)
         def _(k):
-            to = peer(N - k)
-            rows16[to, first:last, :] = ready_rows(to)
+            to = peer(k)
+            rows16[to, first:last, :] = ready_rows(to, first, last)
             send(
-                rows16.at[to, pl.ds(first, last - first)],
-                ready.at[pl.ds(first, last - first), mine],
-                send_sem.at[3],
-                recv_sem.at[3],
-                {"ep": e, "fsdp": to},
+                rows16.at[to, rows], ready.at[rows, mine], send_sem.at[3], recv_sem.at[number], {"ep": e, "fsdp": to}
             ).start()
 
-        ready[first:last, mine] = ready_rows(f)
+    for i in range(len(CUTS) - 1):
+        exact(HALF + 1, N, max(CUTS[i], EARLY[1]), CUTS[i + 1], 3)
+        exact(1, HALF, CUTS[i], CUTS[i + 1], 6)
+    ready[:, mine] = ready_rows(f, 0, ROWS)
 
     drain(columns.at[pl.ds(0, EP - 1)], recv_sem.at[2])
     for k in range(N):
         router[:, 128 * k : 128 * k + 128] = columns[:, k, :].astype(jnp.bfloat16)
 
-    drain(rows16.at[pl.ds(0, N - 1)], recv_sem.at[3])
+    drain(coded.at[0], recv_sem.at[5])
+    drain(coded.at[pl.ds(0, HALF - 1), pl.ds(0, EARLY[1])], recv_sem.at[4])
+
+    def place(source, last):
+        at = pl.ds(pl.multiple_of(source * COLS, COLS), COLS)
+        for k, start, n in blocks_of(0, last):
+            factor = jnp.sqrt(jnp.maximum(parts[source, k : k + 1, :], TINY)) * inverse[k : k + 1, :] * (1.0 / SPREAD)
+            ready[128 * k : 128 * k + n, at] = decode(coded[source, 128 * k : 128 * k + n, :], to_column(factor, start, n))
+
+    place(partner, ROWS)
+
+    @pl.loop(HALF + 1, N)
+    def _(k):
+        place(peer(k), EARLY[1])
+
+    far, near = ROWS - EARLY[1], HALF - 1
+    drain(rows16.at[pl.ds(0, near), pl.ds(0, far)], recv_sem.at[3])
+    drain(rows16.at[pl.ds(0, near)], recv_sem.at[6])
     drain(parts.at[pl.ds(0, N - 1)], send_sem.at[0])
     drain(inverses.at[pl.ds(0, N - 1)], send_sem.at[1])
     drain(columns.at[pl.ds(0, EP - 1)], send_sem.at[2])
@@ -190,9 +267,11 @@
             pltpu.VMEM((N, 8, 128), jnp.float32),
             pltpu.VMEM((EP, N, 128), jnp.float32),
             pltpu.VMEM((N, ROWS, COLS), jnp.bfloat16),
+            pltpu.VMEM((N, ROWS, COLS), jnp.bfloat16),
             pltpu.SemaphoreType.DMA((N + 2,)),
             pltpu.SemaphoreType.DMA((4,)),
-            pltpu.SemaphoreType.DMA((4,)),
+            pltpu.SemaphoreType.DMA((7,)),
+            pltpu.SemaphoreType.REGULAR,
         ],
         compiler_params=pltpu.CompilerParams(
             collective_id=0, has_side_effects=True, vmem_limit_bytes=32 * 2**20

time: 117 us -> 110 us (0.940)
  Pallas kernels: 117 us -> 109 us
    pallas_call x1, Pallas kernels: 115 us -> 107 us  [body(): pl.pallas_call(exchange, out_shape=(jax.ShapeDtypeStruct((ROWS, N * COLS)...]
where the time goes in v2:
time: 110 us
  Pallas kernels  109 us (99%)
    pallas_call x1, Pallas kernels, body(): pl.pallas_call(exchange, out_shape=(jax.ShapeDtypeStruct((ROWS, N * COLS)...  107 us

profile of v2, /device:TPU:8, one launch (start us, length us, event | category | flops | bytes accessed | tf_op | source)
XLA Modules:
  0.0 109.9 jit_solution(14529944099210821670)
XLA Ops:
  0.6 107.3 %exchange.1 = (bf16[448,4096]{1,0:T(8,128)(2,1)S(1)}, f32[1,448]{1,0:T(1,128)S(1)}, bf16[8,4096]{1,0:T(8,128)(2,1)S(1)}) custom-call(f32[32,448,128]{2,1,0:T(8,128)} %bitcast.5, f32[1,128]{1,0:T(1,128)} %bitcast.6, f32[1,128]{1,0:T(1,128)} %bitcast.7), custom_call_target="tpu_custom_call" | custom-call | tf_op jit(solution)/shard_map/exchange/pallas_call | solution.py:252
  107.9 1.9 %store.1 = (bf16[448,4096]{1,0:T(8,128)(2,1)}, f32[1,448]{1,0:T(1,128)}, bf16[8,4096]{1,0:T(8,128)(2,1)}) custom-call(bf16[448,4096]{1,0:T(8,128)(2,1)S(1)} %get-tuple-element.9.ready, f32[1,448]{1,0:T(1,128)S(1)} %get-tuple-element.10.scale, bf16[8,4096]{1,0:T(8,128)(2,1)S(1)} %get-tuple-element.11.router), custom_call_target="tpu_custom_call" | custom-call | tf_op jit(solution)/shard_map/store/pallas_call | solution.py:290

commit v3 on v2

v3 whole, which is shorter than its diff:
```python
import jax
import jax.numpy as jnp
from jax import lax
from jax.experimental import pallas as pl
from jax.experimental.pallas import tpu as pltpu
from jax.sharding import PartitionSpec as P

MESH = pl.DeviceIdType.MESH
N = 32
EP = 8
ROWS = 448
COLS = 128
STORES = 7
HALF = N // 2
CUTS = (0, 128, 256, 384, 448)
EARLY = (16, 96)
POWER = 15
SPREAD = 2.0**8.4
TINY = 1e-37


def peer(k):
    f = lax.axis_index("fsdp")
    h = (f // 16 + k // 16) % 2
    y = ((f // 4) % 4 + (k // 4) % 4) % 4
    x = (f % 4 + k % 4) % 4
    return h * 16 + y * 4 + x


def send(src, dst, send_sem, recv_sem, device):
    return pltpu.make_async_remote_copy(
        src_ref=src,
        dst_ref=dst,
        send_sem=send_sem,
        recv_sem=recv_sem,
        device_id=device,
        device_id_type=MESH,
    )


def drain(ref, sem):
    pltpu.make_async_copy(ref, ref, sem).wait()


def eye():
    return lax.broadcasted_iota(jnp.int32, (128, 128), 0) == lax.broadcasted_iota(jnp.int32, (128, 128), 1)


def to_lanes(column):
    n = column.shape[0]
    return jnp.sum(jnp.where(eye()[:n], column, 0.0), axis=0, keepdims=True)


def to_column(row, start, n):
    return jnp.sum(jnp.where(eye()[start : start + n], row, 0.0), axis=1, keepdims=True)


def code(block, squares):
    u = block * (lax.rsqrt(jnp.maximum(squares, TINY)) * SPREAD)
    u2 = u * u
    u4 = u2 * u2
    return (u4 * u4 * u4 * u2 * u).astype(jnp.bfloat16)


def decode(coded, factor):
    y = coded.astype(jnp.float32)
    size = jnp.exp(jnp.log(jnp.maximum(jnp.abs(y), TINY)) * (1.0 / POWER)) * factor
    return jnp.where(y > 0.0, size, jnp.where(y < 0.0, -size, 0.0 * factor)).astype(jnp.bfloat16)


def blocks_of(first, last):
    row = first
    while row < last:
        k, start = row // 128, row % 128
        n = min(128 - start, last - row)
        yield k, start, n
        row += n


def stacked(blocks):
    return jnp.concatenate(blocks, axis=0) if len(blocks) > 1 else blocks[0]


def exchange(
    train, weight, gain, ready, scale, router,
    x, small, part, parts, norms, routed, sums, others, news, told, rows16, coded,
    load_sem, send_sem, recv_sem, far_sem,
):
    e, f = lax.axis_index("ep"), lax.axis_index("fsdp")
    half, place = f // HALF, f % HALF
    partner = peer(HALF)

    def to(device):
        return {"ep": e, "fsdp": device}

    barrier = pltpu.get_barrier_semaphore()

    @pl.loop(1, HALF + 1)
    def _(k):
        pl.semaphore_signal(barrier, inc=1, device_id=to(peer(k)), device_id_type=MESH)

    @pl.loop(1, EP)
    def _(k):
        pl.semaphore_signal(barrier, inc=1, device_id={"ep": (e + k) % EP, "fsdp": f}, device_id_type=MESH)

    def load(d):
        return pltpu.make_async_copy(train.at[d], x.at[d], load_sem.at[d])

    @pl.loop(0, N)
    def _(k):
        load(peer((HALF + k) % N)).start()

    loads = [pltpu.make_async_copy(ref, small.at[k], load_sem.at[N + k]) for k, ref in enumerate((weight, gain))]
    for copy in loads:
        copy.start()
    for copy in loads:
        copy.wait()
    mine = (small[0] * small[1]).astype(jnp.bfloat16).astype(jnp.float32)
    routed[pl.ds(e, 1), :] = mine

    def squares(d, coded_rows):
        load(d).wait()
        lanes = []
        for k in range(4):
            block = x[d, 128 * k : min(128 * k + 128, ROWS), :]
            column = jnp.sum(block * block, axis=1, keepdims=True)
            lanes.append(to_lanes(column))
            n = min(coded_rows - 128 * k, block.shape[0])
            if n > 0:
                rows16[d, 128 * k : 128 * k + n, :] = code(block[:n], column[:n])
        part[d // HALF, d % HALF] = jnp.concatenate(lanes, axis=0)

    squares(partner, ROWS)

    @pl.loop(HALF + 1, N)
    def _(k):
        squares(peer(k), EARLY[-1])

    pl.semaphore_wait(barrier, HALF + EP - 1)

    pl.semaphore_signal(far_sem, inc=1, device_id=to(partner), device_id_type=MESH)
    send(part.at[partner // HALF, partner % HALF], norms.at[place], send_sem.at[4], recv_sem.at[8], to(partner)).start()
    send(rows16.at[partner], coded.at[place], send_sem.at[3], recv_sem.at[7], to(partner)).start()

    @pl.loop(0, HALF)
    def _(k):
        squares(peer(k), 0)

    @pl.loop(1, HALF)
    def _(k):
        d = peer(k)
        send(part.at[:, d % HALF], parts.at[:, place], send_sem.at[0], recv_sem.at[0], to(d)).start()

    @pl.loop(1, EP)
    def _(k):
        send(
            routed.at[pl.ds(e, 1)], routed.at[pl.ds(e, 1)], send_sem.at[5], recv_sem.at[5], {"ep": (e + k) % EP, "fsdp": f}
        ).start()

    def early(begin, end):
        rows = pl.ds(begin, end - begin)

        @pl.loop(HALF + 1, N)
        def _(k):
            d = peer(k)
            send(rows16.at[d, rows], coded.at[place, rows], send_sem.at[3], recv_sem.at[4], to(d)).start()
            if begin == 0:
                row = pl.ds(0, 1)
                send(part.at[d // HALF, d % HALF, row], norms.at[place, row], send_sem.at[4], recv_sem.at[6], to(d)).start()

    pl.semaphore_wait(far_sem, 1)
    early(0, EARLY[0])

    parts[:, place] = part[:, place]
    drain(parts.at[:, pl.ds(0, HALF - 1)], recv_sem.at[0])
    plane = jnp.sum(parts[...], axis=1)
    sums[0:4, :] = plane[0]
    sums[4:8, :] = plane[1]
    drain(routed.at[pl.ds(0, EP - 1)], recv_sem.at[5])
    sums[8:16, :] = routed[...]
    send(sums, others, send_sem.at[1], recv_sem.at[1], to(partner)).start()

    early(EARLY[0], EARLY[1])
    drain(sums, recv_sem.at[1])
    root = jnp.sqrt(sums[0:8, :] + others[0:8, :])
    news[0:8, :] = 1.0 / root
    first = half == 0
    news[8:16, :] = jnp.where(first, sums[8:16, :], others[8:16, :])
    news[16:24, :] = jnp.where(first, others[8:16, :], sums[8:16, :])

    @pl.loop(1, HALF)
    def _(k):
        send(news, told.at[place], send_sem.at[2], recv_sem.at[2], to(peer(k))).start()

    told[place] = news[...]
    own = jnp.where(first, root[0:4], root[4:8])
    for k in range(4):
        n = min(128, ROWS - 128 * k)
        scale[:, 128 * k : 128 * k + n] = own[k : k + 1, :n]

    drain(told.at[pl.ds(0, HALF - 1)], recv_sem.at[2])

    columns = pl.ds(pl.multiple_of(f * COLS, COLS), COLS)

    def ready_rows(d, first, last):
        return stacked(
            [
                (
                    x[d, 128 * k + start : 128 * k + start + n, :]
                    * to_column(told[d % HALF, pl.ds(4 * (d // HALF) + k, 1), :], start, n)
                ).astype(jnp.bfloat16)
                for k, start, n in blocks_of(first, last)
            ]
        )

    def exact(begin, end, first, last, number):
        rows = pl.ds(first, last - first)

        @pl.loop(begin, end)
        def _(k):
            d = peer(k)
            rows16[d, first:last, :] = ready_rows(d, first, last)
            send(rows16.at[d, rows], ready.at[rows, columns], send_sem.at[3], recv_sem.at[number], to(d)).start()

    for i in range(len(CUTS) - 1):
        exact(HALF + 1, N, max(CUTS[i], EARLY[1]), CUTS[i + 1], 3)
        exact(1, HALF, CUTS[i], CUTS[i + 1], 9)
    ready[:, columns] = ready_rows(f, 0, ROWS)

    for h in range(2):
        for p in range(HALF):
            at = COLS * (HALF * h + p)
            router[:, at : at + COLS] = told[p, 8 + 8 * h : 16 + 8 * h, :].astype(jnp.bfloat16)

    inverse = 1.0 / own

    def decoded(d, last):
        p = d % HALF
        at = pl.ds(pl.multiple_of(d * COLS, COLS), COLS)
        for k, start, n in blocks_of(0, last):
            factor = jnp.sqrt(jnp.maximum(norms[p, k : k + 1, :], TINY)) * inverse[k : k + 1] * (1.0 / SPREAD)
            ready[128 * k : 128 * k + n, at] = decode(coded[p, 128 * k : 128 * k + n, :], to_column(factor, start, n))

    others_far = pl.ds(0, HALF - 1)
    drain(norms.at[0], recv_sem.at[8])
    drain(coded.at[0], recv_sem.at[7])
    decoded(partner, ROWS)
    drain(norms.at[others_far, pl.ds(0, 1)], recv_sem.at[6])
    drain(coded.at[others_far, pl.ds(0, EARLY[1])], recv_sem.at[4])

    @pl.loop(HALF + 1, N)
    def _(k):
        decoded(peer(k), EARLY[1])

    drain(rows16.at[others_far, pl.ds(0, ROWS - EARLY[1])], recv_sem.at[3])
    drain(rows16.at[others_far], recv_sem.at[9])
    drain(parts.at[:, pl.ds(0, HALF - 1)], send_sem.at[0])
    drain(sums, send_sem.at[1])
    drain(told.at[pl.ds(0, HALF - 1)], send_sem.at[2])
    drain(rows16.at[pl.ds(0, N - 1)], send_sem.at[3])
    drain(norms.at[0], send_sem.at[4])
    drain(norms.at[others_far, pl.ds(0, 1)], send_sem.at[4])
    drain(routed.at[pl.ds(0, EP - 1)], send_sem.at[5])


def store(ready, scale, router, ready_out, scale_out, router_out, sem):
    rows = ROWS // STORES
    copies = [pltpu.make_async_copy(scale, scale_out, sem.at[0]), pltpu.make_async_copy(router, router_out, sem.at[1])]
    for k in range(STORES):
        piece = pl.ds(rows * k, rows)
        copies.append(pltpu.make_async_copy(ready.at[piece], ready_out.at[piece], sem.at[2 + k]))
    for copy in copies:
        copy.start()
    for copy in copies:
        copy.wait()


def body(train_down, router_weight, router_gain):
    ready, scale, router = pl.pallas_call(
        exchange,
        out_shape=(
            jax.ShapeDtypeStruct((ROWS, N * COLS), jnp.bfloat16),
            jax.ShapeDtypeStruct((1, ROWS), jnp.float32),
            jax.ShapeDtypeStruct((EP, N * COLS), jnp.bfloat16),
        ),
        in_specs=[pl.BlockSpec(memory_space=pltpu.HBM)] * 3,
        out_specs=[pl.BlockSpec(memory_space=pltpu.VMEM)] * 3,
        scratch_shapes=[
            pltpu.VMEM((N, ROWS, COLS), jnp.float32),
            pltpu.VMEM((2, 1, COLS), jnp.float32),
            pltpu.VMEM((2, HALF, 4, 128), jnp.float32),
            pltpu.VMEM((2, HALF, 4, 128), jnp.float32),
            pltpu.VMEM((HALF, 4, 128), jnp.float32),
            pltpu.VMEM((EP, COLS), jnp.float32),
            pltpu.VMEM((16, 128), jnp.float32),
            pltpu.VMEM((16, 128), jnp.float32),
            pltpu.VMEM((24, 128), jnp.float32),
            pltpu.VMEM((HALF, 24, 128), jnp.float32),
            pltpu.VMEM((N, ROWS, COLS), jnp.bfloat16),
            pltpu.VMEM((HALF, ROWS, COLS), jnp.bfloat16),
            pltpu.SemaphoreType.DMA((N + 2,)),
            pltpu.SemaphoreType.DMA((6,)),
            pltpu.SemaphoreType.DMA((10,)),
            pltpu.SemaphoreType.REGULAR,
        ],
        compiler_params=pltpu.CompilerParams(
            collective_id=0, has_side_effects=True, vmem_limit_bytes=32 * 2**20
        ),
        name="exchange",
    )(
        *(
            pltpu.with_memory_space_constraint(array, pltpu.HBM)
            for array in (
                train_down.reshape(N, ROWS, COLS),
                router_weight.reshape(1, COLS),
                router_gain.reshape(1, COLS),
            )
        )
    )
    ready, scale, router = pl.pallas_call(
        store,
        out_shape=(
            jax.ShapeDtypeStruct(ready.shape, ready.dtype),
            jax.ShapeDtypeStruct(scale.shape, scale.dtype),
            jax.ShapeDtypeStruct(router.shape, router.dtype),
        ),
        in_specs=[pl.BlockSpec(memory_space=pltpu.VMEM)] * 3,
        out_specs=[pl.BlockSpec(memory_space=pltpu.HBM)] * 3,
        scratch_shapes=[pltpu.SemaphoreType.DMA((2 + STORES,))],
        compiler_params=pltpu.CompilerParams(vmem_limit_bytes=2**20),
        name="store",
    )(ready, scale, router)
    return ready[None], scale, router.T


def solution(mesh):
    in_specs = (P("ep", None, "fsdp"), P("fsdp", "ep"), P("fsdp"))
    out_specs = (P("ep", "fsdp", None), P("ep", "fsdp"), P())
    return jax.shard_map(body, mesh=mesh, in_specs=in_specs, out_specs=out_specs, check_vma=False)
```

time: 110 us -> 101 us (0.918)
  Pallas kernels: 109 us -> 99.7 us
    pallas_call x1, Pallas kernels: 107 us -> 97.8 us  [body(): pl.pallas_call(exchange, out_shape=(jax.ShapeDtypeStruct((ROWS, N * COLS)...]
where the time goes in v3:
time: 101 us; the launch traced here: 100 us
  Pallas kernels  99.7 us (99%)
    pallas_call x1, Pallas kernels, body(): pl.pallas_call(exchange, out_shape=(jax.ShapeDtypeStruct((ROWS, N * COLS)...  97.8 us

profile of v3, /device:TPU:8, one launch (start us, length us, event | category | flops | bytes accessed | tf_op | source)
XLA Modules:
  0.0 100.4 jit_solution(9282624739390527838)
XLA Ops:
  0.6 97.8 %exchange.1 = (bf16[448,4096]{1,0:T(8,128)(2,1)S(1)}, f32[1,448]{1,0:T(1,128)S(1)}, bf16[8,4096]{1,0:T(8,128)(2,1)S(1)}) custom-call(f32[32,448,128]{2,1,0:T(8,128)} %bitcast.5, f32[1,128]{1,0:T(1,128)} %bitcast.6, f32[1,128]{1,0:T(1,128)} %bitcast.7), custom_call_target="tpu_custom_call" | custom-call | tf_op jit(solution)/shard_map/exchange/pallas_call | solution.py:279
  98.4 1.9 %store.1 = (bf16[448,4096]{1,0:T(8,128)(2,1)}, f32[1,448]{1,0:T(1,128)}, bf16[8,4096]{1,0:T(8,128)(2,1)}) custom-call(bf16[448,4096]{1,0:T(8,128)(2,1)S(1)} %get-tuple-element.9.ready, f32[1,448]{1,0:T(1,128)S(1)} %get-tuple-element.10.scale, bf16[8,4096]{1,0:T(8,128)(2,1)S(1)} %get-tuple-element.11.router), custom_call_target="tpu_custom_call" | custom-call | tf_op jit(solution)/shard_map/store/pallas_call | solution.py:320

commit v4 on v3

--- a/solution.py
+++ b/solution.py
@@ -12,8 +12,8 @@
 COLS = 128
 STORES = 7
 HALF = N // 2
-CUTS = (0, 128, 256, 384, 448)
-EARLY = (16, 96)
+CUTS = (0, 256, 448)
+EARLY = (48, 112)
 POWER = 15
 SPREAD = 2.0**8.4
 TINY = 1e-37
@@ -93,30 +93,27 @@
     def to(device):
         return {"ep": e, "fsdp": device}
 
-    barrier = pltpu.get_barrier_semaphore()
-
-    @pl.loop(1, HALF + 1)
-    def _(k):
-        pl.semaphore_signal(barrier, inc=1, device_id=to(peer(k)), device_id_type=MESH)
-
-    @pl.loop(1, EP)
-    def _(k):
-        pl.semaphore_signal(barrier, inc=1, device_id={"ep": (e + k) % EP, "fsdp": f}, device_id_type=MESH)
-
     def load(d):
         return pltpu.make_async_copy(train.at[d], x.at[d], load_sem.at[d])
 
-    @pl.loop(0, N)
-    def _(k):
-        load(peer((HALF + k) % N)).start()
-
+    load(partner).start()
     loads = [pltpu.make_async_copy(ref, small.at[k], load_sem.at[N + k]) for k, ref in enumerate((weight, gain))]
     for copy in loads:
         copy.start()
-    for copy in loads:
-        copy.wait()
-    mine = (small[0] * small[1]).astype(jnp.bfloat16).astype(jnp.float32)
-    routed[pl.ds(e, 1), :] = mine
+
+    barrier = pltpu.get_barrier_semaphore()
+
+    @pl.loop(1, HALF + 1)
+    def _(k):
+        pl.semaphore_signal(barrier, inc=1, device_id=to(peer(k)), device_id_type=MESH)
+
+    @pl.loop(1, EP)
+    def _(k):
+        pl.semaphore_signal(barrier, inc=1, device_id={"ep": (e + k) % EP, "fsdp": f}, device_id_type=MESH)
+
+    @pl.loop(1, N)
+    def _(k):
+        load(peer((HALF + k) % N)).start()
 
     def squares(d, coded_rows):
         load(d).wait()
@@ -132,19 +129,24 @@
 
     squares(partner, ROWS)
 
-    @pl.loop(HALF + 1, N)
-    def _(k):
-        squares(peer(k), EARLY[-1])
-
     pl.semaphore_wait(barrier, HALF + EP - 1)
 
     pl.semaphore_signal(far_sem, inc=1, device_id=to(partner), device_id_type=MESH)
     send(part.at[partner // HALF, partner % HALF], norms.at[place], send_sem.at[4], recv_sem.at[8], to(partner)).start()
     send(rows16.at[partner], coded.at[place], send_sem.at[3], recv_sem.at[7], to(partner)).start()
 
+    @pl.loop(HALF + 1, N)
+    def _(k):
+        squares(peer(k), EARLY[-1])
+
     @pl.loop(0, HALF)
     def _(k):
         squares(peer(k), 0)
+
+    for copy in loads:
+        copy.wait()
+    mine = (small[0] * small[1]).astype(jnp.bfloat16).astype(jnp.float32)
+    routed[pl.ds(e, 1), :] = mine
 
     @pl.loop(1, HALF)
     def _(k):

time: 101 us -> 97.9 us (0.969)
  Pallas kernels: 99.7 us -> 97.2 us
    pallas_call x1, Pallas kernels: 97.8 us -> 95.2 us  [body(): pl.pallas_call(exchange, out_shape=(jax.ShapeDtypeStruct((ROWS, N * COLS)...]
where the time goes in v4:
time: 97.9 us; the launch traced here: 97.8 us
  Pallas kernels  97.2 us (99%)
    pallas_call x1, Pallas kernels, body(): pl.pallas_call(exchange, out_shape=(jax.ShapeDtypeStruct((ROWS, N * COLS)...  95.2 us

profile of v4, /device:TPU:8, one launch (start us, length us, event | category | flops | bytes accessed | tf_op | source)
XLA Modules:
  0.0 97.8 jit_solution(13474108433555723029)
XLA Ops:
  0.6 95.2 %exchange.1 = (bf16[448,4096]{1,0:T(8,128)(2,1)S(1)}, f32[1,448]{1,0:T(1,128)S(1)}, bf16[8,4096]{1,0:T(8,128)(2,1)S(1)}) custom-call(f32[32,448,128]{2,1,0:T(8,128)} %bitcast.5, f32[1,128]{1,0:T(1,128)} %bitcast.6, f32[1,128]{1,0:T(1,128)} %bitcast.7), custom_call_target="tpu_custom_call" | custom-call | tf_op jit(solution)/shard_map/exchange/pallas_call | solution.py:281
  95.9 1.9 %store.1 = (bf16[448,4096]{1,0:T(8,128)(2,1)}, f32[1,448]{1,0:T(1,128)}, bf16[8,4096]{1,0:T(8,128)(2,1)}) custom-call(bf16[448,4096]{1,0:T(8,128)(2,1)S(1)} %get-tuple-element.9.ready, f32[1,448]{1,0:T(1,128)S(1)} %get-tuple-element.10.scale, bf16[8,4096]{1,0:T(8,128)(2,1)S(1)} %get-tuple-element.11.router), custom_call_target="tpu_custom_call" | custom-call | tf_op jit(solution)/shard_map/store/pallas_call | solution.py:322

commit v5 on v4

--- a/solution.py
+++ b/solution.py
@@ -13,7 +13,7 @@
 STORES = 7
 HALF = N // 2
 CUTS = (0, 256, 448)
-EARLY = (48, 112)
+EARLY = (64, 112)
 POWER = 15
 SPREAD = 2.0**8.4
 TINY = 1e-37
@@ -103,7 +103,9 @@
 
     barrier = pltpu.get_barrier_semaphore()
 
-    @pl.loop(1, HALF + 1)
+    pl.semaphore_signal(barrier, inc=1, device_id=to(partner), device_id_type=MESH)
+
+    @pl.loop(1, HALF)
     def _(k):
         pl.semaphore_signal(barrier, inc=1, device_id=to(peer(k)), device_id_type=MESH)
 

time: 97.9 us -> 97.6 us (level)
  no operation moved by 1% of the time
where the time goes in v5:
time: 97.6 us; the launch traced here: 97.2 us
  Pallas kernels  96.5 us (99%)
    pallas_call x1, Pallas kernels, body(): pl.pallas_call(exchange, out_shape=(jax.ShapeDtypeStruct((ROWS, N * COLS)...  94.6 us

profile of v5, /device:TPU:8, one launch (start us, length us, event | category | flops | bytes accessed | tf_op | source)
XLA Modules:
  0.0 97.2 jit_solution(6389887085434144983)
XLA Ops:
  0.6 94.6 %exchange.1 = (bf16[448,4096]{1,0:T(8,128)(2,1)S(1)}, f32[1,448]{1,0:T(1,128)S(1)}, bf16[8,4096]{1,0:T(8,128)(2,1)S(1)}) custom-call(f32[32,448,128]{2,1,0:T(8,128)} %bitcast.5, f32[1,128]{1,0:T(1,128)} %bitcast.6, f32[1,128]{1,0:T(1,128)} %bitcast.7), custom_call_target="tpu_custom_call" | custom-call | tf_op jit(solution)/shard_map/exchange/pallas_call | solution.py:283
  95.2 1.9 %store.1 = (bf16[448,4096]{1,0:T(8,128)(2,1)}, f32[1,448]{1,0:T(1,128)}, bf16[8,4096]{1,0:T(8,128)(2,1)}) custom-call(bf16[448,4096]{1,0:T(8,128)(2,1)S(1)} %get-tuple-element.9.ready, f32[1,448]{1,0:T(1,128)S(1)} %get-tuple-element.10.scale, bf16[8,4096]{1,0:T(8,128)(2,1)S(1)} %get-tuple-element.11.router), custom_call_target="tpu_custom_call" | custom-call | tf_op jit(solution)/shard_map/store/pallas_call | solution.py:324

commit v6 on v5

--- a/solution.py
+++ b/solution.py
@@ -228,6 +228,7 @@
 
     for i in range(len(CUTS) - 1):
         exact(HALF + 1, N, max(CUTS[i], EARLY[1]), CUTS[i + 1], 3)
+    for i in range(len(CUTS) - 1):
         exact(1, HALF, CUTS[i], CUTS[i + 1], 9)
     ready[:, columns] = ready_rows(f, 0, ROWS)
 

time: 97.6 us -> 97.6 us (level)
  no operation moved by 1% of the time
where the time goes in v6:
time: 97.6 us; the launch traced here: 97.2 us
  Pallas kernels  96.5 us (99%)
    pallas_call x1, Pallas kernels, body(): pl.pallas_call(exchange, out_shape=(jax.ShapeDtypeStruct((ROWS, N * COLS)...  94.6 us

profile of v6, /device:TPU:8, one launch (start us, length us, event | category | flops | bytes accessed | tf_op | source)
XLA Modules:
  0.0 97.2 jit_solution(3635070068687662166)
XLA Ops:
  0.6 94.6 %exchange.1 = (bf16[448,4096]{1,0:T(8,128)(2,1)S(1)}, f32[1,448]{1,0:T(1,128)S(1)}, bf16[8,4096]{1,0:T(8,128)(2,1)S(1)}) custom-call(f32[32,448,128]{2,1,0:T(8,128)} %bitcast.5, f32[1,128]{1,0:T(1,128)} %bitcast.6, f32[1,128]{1,0:T(1,128)} %bitcast.7), custom_call_target="tpu_custom_call" | custom-call | tf_op jit(solution)/shard_map/exchange/pallas_call | solution.py:284
  95.2 1.9 %store.1 = (bf16[448,4096]{1,0:T(8,128)(2,1)}, f32[1,448]{1,0:T(1,128)}, bf16[8,4096]{1,0:T(8,128)(2,1)}) custom-call(bf16[448,4096]{1,0:T(8,128)(2,1)S(1)} %get-tuple-element.9.ready, f32[1,448]{1,0:T(1,128)S(1)} %get-tuple-element.10.scale, bf16[8,4096]{1,0:T(8,128)(2,1)S(1)} %get-tuple-element.11.router), custom_call_target="tpu_custom_call" | custom-call | tf_op jit(solution)/shard_map/store/pallas_call | solution.py:325

commit v7 on v5

--- a/solution.py
+++ b/solution.py
@@ -13,7 +13,7 @@
 STORES = 7
 HALF = N // 2
 CUTS = (0, 256, 448)
-EARLY = (64, 112)
+EARLY = (64, 96)
 POWER = 15
 SPREAD = 2.0**8.4
 TINY = 1e-37

time: 97.6 us -> 99.1 us (1.015)
  Pallas kernels: 96.5 us -> 98.1 us
    pallas_call x1, Pallas kernels: 94.6 us -> 96.2 us  [body(): pl.pallas_call(exchange, out_shape=(jax.ShapeDtypeStruct((ROWS, N * COLS)...]
where the time goes in v7:
time: 99.1 us; the launch traced here: 98.8 us
  Pallas kernels  98.1 us (99%)
    pallas_call x1, Pallas kernels, body(): pl.pallas_call(exchange, out_shape=(jax.ShapeDtypeStruct((ROWS, N * COLS)...  96.2 us

profile of v7, /device:TPU:8, one launch (start us, length us, event | category | flops | bytes accessed | tf_op | source)
XLA Modules:
  0.0 98.8 jit_solution(17645242705495896087)
XLA Ops:
  0.6 96.2 %exchange.1 = (bf16[448,4096]{1,0:T(8,128)(2,1)S(1)}, f32[1,448]{1,0:T(1,128)S(1)}, bf16[8,4096]{1,0:T(8,128)(2,1)S(1)}) custom-call(f32[32,448,128]{2,1,0:T(8,128)} %bitcast.5, f32[1,128]{1,0:T(1,128)} %bitcast.6, f32[1,128]{1,0:T(1,128)} %bitcast.7), custom_call_target="tpu_custom_call" | custom-call | tf_op jit(solution)/shard_map/exchange/pallas_call | solution.py:283
  96.8 1.9 %store.1 = (bf16[448,4096]{1,0:T(8,128)(2,1)}, f32[1,448]{1,0:T(1,128)}, bf16[8,4096]{1,0:T(8,128)(2,1)}) custom-call(bf16[448,4096]{1,0:T(8,128)(2,1)S(1)} %get-tuple-element.9.ready, f32[1,448]{1,0:T(1,128)S(1)} %get-tuple-element.10.scale, bf16[8,4096]{1,0:T(8,128)(2,1)S(1)} %get-tuple-element.11.router), custom_call_target="tpu_custom_call" | custom-call | tf_op jit(solution)/shard_map/store/pallas_call | solution.py:324
